TPU v7x, 32 devices: a whole 2x2x4 slice. The times are simulated.
32 devices in a mesh: img: 4 (over x, core), slab: 8 (over z, y).
Axes of the slice: x: 2, y: 2, z: 4, core: 2. Of those that a mesh axis runs over, the one named last changes fastest.
Arguments:
- section_input: bfloat16 [256, 256, 1024], P(('img', 'slab')), parts along dimension 0, may hold values from -54 to 54
- w_reduce: bfloat16 [3, 1024, 256], replicated, may hold values from -0.1875 to 0.1875
- w_spatial: bfloat16 [3, 9, 256, 256], replicated, may hold values from -0.125 to 0.125
- w_expand: bfloat16 [3, 256, 1024], replicated, may hold values from -0.375 to 0.375
- gain_mid: float32 [3, 2, 256], replicated, may hold values from 0.25 to 1.75
- shift_mid: float32 [3, 2, 256], replicated, may hold values from -3 to 3
- gain_out: float32 [3, 1024], replicated, may hold values from 0.25 to 1.75
- shift_out: float32 [3, 1024], replicated, may hold values from -3 to 3
Outputs:
- section_output: bfloat16 [256, 256, 1024], P(('img', 'slab')), parts along dimension 0
There are 4 independent parts, one for each index of `img`. A program takes and returns all parts, laid end to end along the dimension named above; an argument that names none is the same for every part. Nothing has to cross between parts.
All inputs are finite; a program needn't handle non-finite values.
Results may differ from a plain program's by a relative error of at most 0.01.
Values may be sent and summed in bfloat16 or wider, within the bound.
A program may use at most 128 MiB of HBM per device.

v0:
```python
import jax
import jax.numpy as jnp
from jax import lax
from jax.sharding import PartitionSpec as P


def with_halo(block, sides, width):
    for axis, dim in sides:
        count = lax.axis_size(axis)
        forward = [(i, i + 1) for i in range(count - 1)]
        backward = [(target, source) for source, target in forward]
        low = lax.ppermute(
            lax.slice_in_dim(block, block.shape[dim] - width, None, axis=dim), axis, forward
        )
        high = lax.ppermute(lax.slice_in_dim(block, 0, width, axis=dim), axis, backward)
        block = jnp.concatenate([low, block, high], axis=dim)
    return block


def batch_stats(values, count):
    total, squares = lax.psum((jnp.sum(values, axis=0), jnp.sum(values * values, axis=0)), "slab")
    mean = total / count
    var = jnp.maximum(squares / count - mean * mean, 0.0)
    return (mean, lax.rsqrt(var + 1e-05))


def spatial_conv(padded_rows, taps, rows, width):
    mid = padded_rows.shape[2]
    padded = jnp.pad(padded_rows, ((0, 0), (1, 1), (0, 0)))
    total = jnp.zeros((rows * width, taps.shape[2]), jnp.float32)
    for down in range(3):
        for across in range(3):
            window = padded[down : down + rows, across : across + width].reshape(-1, mid)
            total = total + jnp.dot(
                window, taps[3 * down + across], preferred_element_type=jnp.float32
            )
    return total


def local(section_input, w_reduce, w_spatial, w_expand, gain_mid, shift_mid, gain_out, shift_out):
    rows, width, chans = section_input.shape
    mid = w_reduce.shape[2]
    slabs = lax.axis_size("slab")
    place = lax.axis_index("slab")
    count = float(rows * width * slabs)
    current = section_input
    for layer in range(w_reduce.shape[0]):
        flat = current.reshape(-1, chans)
        gain_one = gain_mid[layer, 0]
        shift_one = shift_mid[layer, 0]
        extended = with_halo(current, (("slab", 0),), 1)
        reduced = jnp.dot(
            extended.reshape(-1, chans), w_reduce[layer], preferred_element_type=jnp.float32
        )
        reduced = reduced.reshape(rows + 2, width, mid)
        mean, scale = batch_stats(reduced[1:-1].reshape(-1, mid), count)
        hidden = jnp.maximum((reduced - mean) * scale * gain_one + shift_one, 0.0)
        above = jnp.where(place == 0, 0.0, 1.0).astype(jnp.float32)
        below = jnp.where(place == slabs - 1, 0.0, 1.0).astype(jnp.float32)
        row_mask = jnp.concatenate([above[None], jnp.ones((rows,), jnp.float32), below[None]])
        padded_rows = (hidden * row_mask[:, None, None]).astype(jnp.bfloat16)
        spatial = spatial_conv(padded_rows, w_spatial[layer], rows, width)
        mean, scale = batch_stats(spatial, count)
        inner = jnp.maximum(
            (spatial - mean) * scale * gain_mid[layer, 1] + shift_mid[layer, 1], 0.0
        ).astype(jnp.bfloat16)
        expanded = jnp.dot(inner, w_expand[layer], preferred_element_type=jnp.float32)
        mean, scale = batch_stats(expanded, count)
        summed = (
            (expanded - mean) * scale * gain_out[layer]
            + shift_out[layer]
            + flat.astype(jnp.float32)
        )
        current = jnp.maximum(summed, 0.0).astype(jnp.bfloat16).reshape(rows, width, chans)
    return current


def solution(mesh):
    placed = (P(("img", "slab"), None, None), P(), P(), P(), P(), P(), P(), P())
    return jax.shard_map(
        local, mesh=mesh, in_specs=placed, out_specs=P(("img", "slab"), None, None), check_vma=False
    )
```

profile of v0, /device:TPU:0, one launch (start us, length us, event | category | flops | bytes accessed | tf_op | source)
XLA Modules:
  0.0 329.2 jit_solution(1371275087114166597)
XLA Ops:
  1.3 4.9 %collective-permute-start = (bf16[1,256,1024]{2,1,0:T(8,128)(2,1)S(1)}, bf16[1,256,1024]{2,1,0:T(8,128)(2,1)S(1)}, u32[]{:S(2)}, u32[]{:S(2)}) collective-permute-start(bf16[1,256,1024]{2,1,0:T(8,128)(2,1)S(1)} %get-tuple-element.45), channel_id=1, source_target_pairs={{0,1},{1,2},{2,3},{3,4},{4,5},{5,6},{6,7},{8,9},{9,10},{10,11},{11... | collective-permute-start | bytes 1572872 | tf_op jit(solution)/shard_map/ppermute | solution.py:12
  10.9 17.7 %collective-permute-done = bf16[1,256,1024]{2,1,0:T(8,128)(2,1)S(1)} collective-permute-done((bf16[1,256,1024]{2,1,0:T(8,128)(2,1)S(1)}, bf16[1,256,1024]{2,1,0:T(8,128)(2,1)S(1)}, u32[]{:S(2)}, u32[]{:S(2)}) %collective-permute-start) | collective-permute-done | bytes 524320 | tf_op jit(solution)/shard_map/ppermute | solution.py:12
  28.6 2.8 pad_maximum_fusion
  31.4 2.6 fusion.27
  34.3 21.6 %all-reduce.11 = (f32[256]{0:T(256)S(1)}, f32[256]{0:T(256)S(1)}) all-reduce(f32[256]{0:T(256)S(1)} %get-tuple-element.16, f32[256]{0:T(256)S(1)} %get-tuple-element.15), channel_id=1, replica_groups=mesh['img'=4,'slab'=8] {'slab'}, use_global_device_ids=true, to_apply=%region_3.0 | all-reduce | flops 512 | bytes 4096 | tf_op jit(solution)/shard_map/psum | solution.py:21
  56.5 4.1 %pad_slice_fusion.12 = (bf16[8,256,256]{2,1,0:T(8,128)(2,1)S(1)}, bf16[8,256,256]{2,1,0:T(8,128)(2,1)S(1)}, bf16[8,256,256]{2,1,0:T(8,128)(2,1)S(1)}, bf16[8,256...) fusion(bf16[10,256,256]{2,1,0:T(8,128)(2,1)S(1)} %multiply_conv, ...), kind=kLoop, calls=%fused_computation.80 | loop fusion | bytes 13893632 | tf_op jit(solution)/shard_map/slice | solution.py:33
  71.5 1.5 fusion.100
  73.0 17.1 %all-reduce.10 = (f32[256]{0:T(256)S(1)}, f32[256]{0:T(256)S(1)}) all-reduce(f32[256]{0:T(256)S(1)} %get-tuple-element.22, f32[256]{0:T(256)S(1)} %get-tuple-element.21), channel_id=1, replica_groups=mesh['img'=4,'slab'=8] {'slab'}, use_global_device_ids=true, to_apply=%region_7.8 | all-reduce | flops 512 | bytes 4096 | tf_op jit(solution)/shard_map/psum | solution.py:21
  90.1 5.8 %fusion.97 = (f32[1024]{0:T(1024)S(1)}, f32[1024]{0:T(1024)S(1)}, f32[2048,1024]{1,0:T(8,128)}) fusion(bf16[3,256,1024]{2,1,0:T(8,128)(2,1)} %param.11, f32[2048,256]{1,0:T(8,128)S(1)} %get-tuple-element.110, f32[256]{0:T(256)S(1)} %bitcast.260, f32[256]{0:T(256)S(1)} %bitcast.259, f32[256]{0:T(256)S(1)} %get-tuple-element.107, f32[256]{0:T(256)S(1)} %get-tuple-element.106), kind=kOutput, calls=%fused_computation.186 | convolution fusion | flops 1083176960 | bytes 11022336 | tf_op jit(solution)/shard_map/dot_general | solution.py:67
  95.9 19.4 %all-reduce.9 = (f32[1024]{0:T(1024)S(1)}, f32[1024]{0:T(1024)S(1)}) all-reduce(f32[1024]{0:T(1024)S(1)} %get-tuple-element.10, f32[1024]{0:T(1024)S(1)} %get-tuple-element.9), channel_id=1, replica_groups=mesh['img'=4,'slab'=8] {'slab'}, use_global_device_ids=true, to_apply=%region_11.12 | all-reduce | flops 2048 | bytes 16384 | tf_op jit(solution)/shard_map/psum | solution.py:21
  115.3 5.7 %fusion.1 = bf16[2048,1024]{1,0:T(8,128)(2,1)S(1)} fusion(f32[2048,1024]{1,0:T(8,128)} %get-tuple-element.111, bf16[8,256,1024]{2,1,0:T(8,128)(2,1)} %param.8, f32[1024]{0:T(1024)S(1)} %bitcast.248, f32[1024]{0:T(1024)S(1)} %bitcast.247, f32[1024]{0:T(1024)S(1)} %get-tuple-element.97, f32[1024]{0:T(1024)S(1)} %get-tuple-element.96), kind=kLoop, calls=%fused_computation.2 | loop fusion | flops 16777216 | bytes 16793600 | tf_op jit(solution)/shard_map/convert_element_type | solution.py:74
  121.1 2.0 collective-permute-start.2
  124.6 11.0 %collective-permute-done.2 = bf16[1,256,1024]{2,1,0:T(8,128)(2,1)S(1)} collective-permute-done((bf16[1,256,1024]{2,1,0:T(8,128)(2,1)S(1)}, bf16[1,256,1024]{2,1,0:T(8,128)(2,1)S(1)}, u32[]{:S(2)}, u32[]{:S(2)}) %collective-permute-start.2) | collective-permute-done | bytes 524320 | tf_op jit(solution)/shard_map/ppermute | solution.py:12
  136.3 2.6 fusion.24
  139.2 19.6 %all-reduce.8 = (f32[256]{0:T(256)S(1)}, f32[256]{0:T(256)S(1)}) all-reduce(f32[256]{0:T(256)S(1)} %get-tuple-element.14, f32[256]{0:T(256)S(1)} %get-tuple-element.13), channel_id=1, replica_groups=mesh['img'=4,'slab'=8] {'slab'}, use_global_device_ids=true, to_apply=%region_15.16 | all-reduce | flops 512 | bytes 4096 | tf_op jit(solution)/shard_map/psum | solution.py:21
  159.4 4.1 %pad_slice_fusion.6 = (bf16[8,256,256]{2,1,0:T(8,128)(2,1)S(1)}, bf16[8,256,256]{2,1,0:T(8,128)(2,1)S(1)}, bf16[8,256,256]{2,1,0:T(8,128)(2,1)S(1)}, bf16[8,256,...) fusion(bf16[10,256,256]{2,1,0:T(8,128)(2,1)S(1)} %multiply_conv, ...), kind=kLoop, calls=%fused_computation.74 | loop fusion | bytes 13893632 | tf_op jit(solution)/shard_map/slice | solution.py:33
  174.4 1.5 fusion.99
  175.9 17.1 %all-reduce.7 = (f32[256]{0:T(256)S(1)}, f32[256]{0:T(256)S(1)}) all-reduce(f32[256]{0:T(256)S(1)} %get-tuple-element.20, f32[256]{0:T(256)S(1)} %get-tuple-element.19), channel_id=1, replica_groups=mesh['img'=4,'slab'=8] {'slab'}, use_global_device_ids=true, to_apply=%region_19.20 | all-reduce | flops 512 | bytes 4096 | tf_op jit(solution)/shard_map/psum | solution.py:21
  193.0 5.8 %fusion.96 = (f32[1024]{0:T(1024)S(1)}, f32[1024]{0:T(1024)S(1)}, f32[2048,1024]{1,0:T(8,128)}) fusion(bf16[3,256,1024]{2,1,0:T(8,128)(2,1)} %param.11, f32[2048,256]{1,0:T(8,128)S(1)} %get-tuple-element.112, f32[256]{0:T(256)S(1)} %bitcast.258, f32[256]{0:T(256)S(1)} %bitcast.257, f32[256]{0:T(256)S(1)} %get-tuple-element.103, f32[256]{0:T(256)S(1)} %get-tuple-element.102), kind=kOutput, calls=%fused_computation.185 | convolution fusion | flops 1083176960 | bytes 11022336 | tf_op jit(solution)/shard_map/dot_general | solution.py:67
  198.8 19.6 %all-reduce.6 = (f32[1024]{0:T(1024)S(1)}, f32[1024]{0:T(1024)S(1)}) all-reduce(f32[1024]{0:T(1024)S(1)} %get-tuple-element.8, f32[1024]{0:T(1024)S(1)} %get-tuple-element.7), channel_id=1, replica_groups=mesh['img'=4,'slab'=8] {'slab'}, use_global_device_ids=true, to_apply=%region_23.24 | all-reduce | flops 2048 | bytes 16384 | tf_op jit(solution)/shard_map/psum | solution.py:21
  218.4 5.7 %maximum_convert_fusion.1 = bf16[2048,1024]{1,0:T(8,128)(2,1)S(1)} fusion(bf16[2048,1024]{1,0:T(8,128)(2,1)} %copy-done.1, f32[2048,1024]{1,0:T(8,128)} %get-tuple-element.113, f32[1024]{0:T(1024)S(1)} %bitcast.246, f32[1024]{0:T(1024)S(1)} %bitcast.245, f32[1024]{0:T(1024)S(1)} %get-tuple-element.95, f32[1024]{0:T(1024)S(1)} %get-tuple-element.94), kind=kLoop, calls=%fused_computation.5 | loop fusion | flops 16777216 | bytes 16793600 | tf_op jit(solution)/shard_map/convert_element_type | solution.py:74
  224.2 3.1 collective-permute-start.4
  227.3 1.5 collective-permute-start.5
  228.8 10.8 %collective-permute-done.4 = bf16[1,256,1024]{2,1,0:T(8,128)(2,1)S(1)} collective-permute-done((bf16[1,256,1024]{2,1,0:T(8,128)(2,1)S(1)}, bf16[1,256,1024]{2,1,0:T(8,128)(2,1)S(1)}, u32[]{:S(2)}, u32[]{:S(2)}) %collective-permute-start.4) | collective-permute-done | bytes 524320 | tf_op jit(solution)/shard_map/ppermute | solution.py:12
  240.3 2.6 fusion.21
  243.2 19.6 %all-reduce.5 = (f32[256]{0:T(256)S(1)}, f32[256]{0:T(256)S(1)}) all-reduce(f32[256]{0:T(256)S(1)} %get-tuple-element.12, f32[256]{0:T(256)S(1)} %get-tuple-element.11), channel_id=1, replica_groups=mesh['img'=4,'slab'=8] {'slab'}, use_global_device_ids=true, to_apply=%region_27.28 | all-reduce | flops 512 | bytes 4096 | tf_op jit(solution)/shard_map/psum | solution.py:21
  263.4 4.1 %pad_slice_fusion = (bf16[8,256,256]{2,1,0:T(8,128)(2,1)S(1)}, bf16[8,256,256]{2,1,0:T(8,128)(2,1)S(1)}, bf16[8,256,256]{2,1,0:T(8,128)(2,1)S(1)}, bf16[8,256,25...) fusion(bf16[10,256,256]{2,1,0:T(8,128)(2,1)S(1)} %multiply_conv, ...), kind=kLoop, calls=%fused_computation.68 | loop fusion | bytes 13893632 | tf_op jit(solution)/shard_map/slice | solution.py:33
  278.4 1.5 fusion.98
  279.9 17.1 %all-reduce.4 = (f32[256]{0:T(256)S(1)}, f32[256]{0:T(256)S(1)}) all-reduce(f32[256]{0:T(256)S(1)} %get-tuple-element.18, f32[256]{0:T(256)S(1)} %get-tuple-element.17), channel_id=1, replica_groups=mesh['img'=4,'slab'=8] {'slab'}, use_global_device_ids=true, to_apply=%region_31.32 | all-reduce | flops 512 | bytes 4096 | tf_op jit(solution)/shard_map/psum | solution.py:21
  297.1 5.8 %fusion.95 = (f32[1024]{0:T(1024)S(1)}, f32[1024]{0:T(1024)S(1)}, f32[2048,1024]{1,0:T(8,128)}) fusion(bf16[3,256,1024]{2,1,0:T(8,128)(2,1)} %param.11, f32[2048,256]{1,0:T(8,128)S(1)} %get-tuple-element.114, f32[256]{0:T(256)S(1)} %bitcast.256, f32[256]{0:T(256)S(1)} %bitcast.255, f32[256]{0:T(256)S(1)} %get-tuple-element.99, f32[256]{0:T(256)S(1)} %get-tuple-element.98), kind=kOutput, calls=%fused_computation.184 | convolution fusion | flops 1083176960 | bytes 11022336 | tf_op jit(solution)/shard_map/dot_general | solution.py:67
  302.8 19.4 %all-reduce.3 = (f32[1024]{0:T(1024)S(1)}, f32[1024]{0:T(1024)S(1)}) all-reduce(f32[1024]{0:T(1024)S(1)} %get-tuple-element.6, f32[1024]{0:T(1024)S(1)} %get-tuple-element.5), channel_id=1, replica_groups=mesh['img'=4,'slab'=8] {'slab'}, use_global_device_ids=true, to_apply=%region_35.36 | all-reduce | flops 2048 | bytes 16384 | tf_op jit(solution)/shard_map/psum | solution.py:21
  322.2 7.0 %maximum_convert_fusion = bf16[2048,1024]{1,0:T(8,128)(2,1)} fusion(bf16[2048,1024]{1,0:T(8,128)(2,1)} %copy-done, f32[2048,1024]{1,0:T(8,128)} %get-tuple-element.115, f32[1024]{0:T(1024)S(1)} %bitcast.244, f32[1024]{0:T(1024)S(1)} %bitcast.243, f32[1024]{0:T(1024)S(1)} %get-tuple-element.93, f32[1024]{0:T(1024)S(1)} %get-tuple-element.92), kind=kLoop, calls=%fused_computation.3 | loop fusion | flops 16777216 | bytes 16793600 | tf_op jit(solution)/shard_map/convert_element_type | solution.py:74
  (59 shorter events, 44.1 us)
Async XLA Ops:
  1.3 27.3 %collective-permute-start = (bf16[1,256,1024]{2,1,0:T(8,128)(2,1)S(1)}, bf16[1,256,1024]{2,1,0:T(8,128)(2,1)S(1)}, u32[]{:S(2)}, u32[]{:S(2)}) collective-permute-start(bf16[1,256,1024]{2,1,0:T(8,128)(2,1)S(1)} %get-tuple-element.45), channel_id=1, source_target_pairs={{0,1},{1,2},{2,3},{3,4},{4,5},{5,6},{6,7},{8,9},{9,10},{10,11},{11... | collective-permute-start | bytes 1572872 | tf_op jit(solution)/shard_map/ppermute | solution.py:12
  6.2 22.4 %collective-permute-start.1 = (bf16[1,256,1024]{2,1,0:T(8,128)(2,1)S(1)}, bf16[1,256,1024]{2,1,0:T(8,128)(2,1)S(1)}, u32[]{:S(2)}, u32[]{:S(2)}) collective-permute-start(bf16[1,256,1024]{2,1,0:T(8,128)(2,1)S(1)} %get-tuple-element.46), channel_id=1, source_target_pairs={{1,0},{2,1},{3,2},{4,3},{5,4},{6,5},{7,6},{9,8},{10,9},{11,10},{12... | collective-permute-start | bytes 1572872 | tf_op jit(solution)/shard_map/ppermute | solution.py:15
  121.0 15.2 %copy-start.1 = (bf16[2048,1024]{1,0:T(8,128)(2,1)}, bf16[2048,1024]{1,0:T(8,128)(2,1)S(1)}, u32[]{:S(2)}) copy-start(bf16[2048,1024]{1,0:T(8,128)(2,1)S(1)} %fusion.1) | copy-start | bytes 12582916
  121.1 14.5 %collective-permute-start.2 = (bf16[1,256,1024]{2,1,0:T(8,128)(2,1)S(1)}, bf16[1,256,1024]{2,1,0:T(8,128)(2,1)S(1)}, u32[]{:S(2)}, u32[]{:S(2)}) collective-permute-start(bf16[1,256,1024]{2,1,0:T(8,128)(2,1)S(1)} %get-tuple-element.43), channel_id=1, source_target_pairs={{0,1},{1,2},{2,3},{3,4},{4,5},{5,6},{6,7},{8,9},{9,10},{10,11},{11... | collective-permute-start | bytes 1572872 | tf_op jit(solution)/shard_map/ppermute | solution.py:12
  123.2 12.4 %collective-permute-start.3 = (bf16[1,256,1024]{2,1,0:T(8,128)(2,1)S(1)}, bf16[1,256,1024]{2,1,0:T(8,128)(2,1)S(1)}, u32[]{:S(2)}, u32[]{:S(2)}) collective-permute-start(bf16[1,256,1024]{2,1,0:T(8,128)(2,1)S(1)} %get-tuple-element.44), channel_id=1, source_target_pairs={{1,0},{2,1},{3,2},{4,3},{5,4},{6,5},{7,6},{9,8},{10,9},{11,10},{12... | collective-permute-start | bytes 1572872 | tf_op jit(solution)/shard_map/ppermute | solution.py:15
  224.1 16.2 %copy-start = (bf16[2048,1024]{1,0:T(8,128)(2,1)}, bf16[2048,1024]{1,0:T(8,128)(2,1)S(1)}, u32[]{:S(2)}) copy-start(bf16[2048,1024]{1,0:T(8,128)(2,1)S(1)} %maximum_convert_fusion.1) | copy-start | bytes 12582916
  224.2 15.5 %collective-permute-start.4 = (bf16[1,256,1024]{2,1,0:T(8,128)(2,1)S(1)}, bf16[1,256,1024]{2,1,0:T(8,128)(2,1)S(1)}, u32[]{:S(2)}, u32[]{:S(2)}) collective-permute-start(bf16[1,256,1024]{2,1,0:T(8,128)(2,1)S(1)} %get-tuple-element.41), channel_id=1, source_target_pairs={{0,1},{1,2},{2,3},{3,4},{4,5},{5,6},{6,7},{8,9},{9,10},{10,11},{11... | collective-permute-start | bytes 1572872 | tf_op jit(solution)/shard_map/ppermute | solution.py:12
  227.3 12.3 %collective-permute-start.5 = (bf16[1,256,1024]{2,1,0:T(8,128)(2,1)S(1)}, bf16[1,256,1024]{2,1,0:T(8,128)(2,1)S(1)}, u32[]{:S(2)}, u32[]{:S(2)}) collective-permute-start(bf16[1,256,1024]{2,1,0:T(8,128)(2,1)S(1)} %get-tuple-element.42), channel_id=1, source_target_pairs={{1,0},{2,1},{3,2},{4,3},{5,4},{6,5},{7,6},{9,8},{10,9},{11,10},{12... | collective-permute-start | bytes 1572872 | tf_op jit(solution)/shard_map/ppermute | solution.py:15
where the time goes:
time: 331 us; the launch traced here: 329 us
  blocking collectives  170 us (51%)
  matrix products  62.1 us (19%)
  waiting for transfers between devices  39.5 us (12%)
  other arithmetic  25.5 us (8%)
  local copies, waits for them, and re-layouts  16.9 us (5%)
  starting transfers between devices  14.4 us (4%)
    psum x9, blocking collectives, batch_stats(): lax.psum((jnp.sum(values, axis=0), jnp.sum(values * values, axis=0)), 'sl...  170 us
    ppermute x3, waiting for transfers between devices, with_halo(): lax.ppermute(lax.slice_in_dim(block, block.shape[dim] - width, None, axis...  39.5 us
    dot_general x27, matrix products, spatial_conv(): jnp.dot(window, taps[3 * down + across], preferred_element_type=jnp.float32)  37 us
    convert_element_type x3, other arithmetic, local(): jnp.maximum(summed, 0.0).astype(jnp.bfloat16).reshape(rows, width, chans)  18.5 us
    dot_general x3, matrix products, local(): jnp.dot(inner, w_expand[layer], preferred_element_type=jnp.float32)  17.3 us
    slice x3, local copies, waits for them, and re-layouts, spatial_conv(): window = padded[down:down + rows, across:across + width].reshape(-1, mid)  12.2 us
    ppermute x3, starting transfers between devices, with_halo(): lax.ppermute(lax.slice_in_dim(block, block.shape[dim] - width, None, axis...  10.1 us
    dot_general x3, matrix products, local(): jnp.dot(extended.reshape(-1, chans), w_reduce[layer], preferred_element_t...  7.86 us
  transfers between devices with their start and end apart: 6, of which 3 were waited for; matrix products, arithmetic and copies ran while one was open for 1% of the time, Pallas kernels for 0%

commit v1 on v0

v1 whole, which is shorter than its diff:
```python
import functools

import jax
import jax.numpy as jnp
from jax import lax
from jax.experimental import pallas as pl
from jax.experimental.pallas import tpu as pltpu
from jax.sharding import PartitionSpec as P

MESH = pl.DeviceIdType.MESH
EPS = 1e-05


def kernel(
    n, x_hbm, wr_hbm, ws_hbm, we_hbm, gain_mid, shift_mid, gain_out, shift_out, out_hbm,
    x, wr, ws, we, red, taps, inner, expanded, halo_out, halo_in, stat_out, stat,
    x_sem, w_sem, out_sem, halo_send, halo_recv, stat_send, stat_recv,
):
    rows, width, chans = x.shape
    layers, _, mid = wr.shape
    chunks = chans // mid
    stages = 2 + chunks
    step = 2 if rows % 2 == 0 else 1
    me = lax.axis_index("slab")
    inv_local = 1.0 / (rows * width)
    inv_count = 1.0 / (rows * width * n)

    def peer(k):
        return lax.rem(me + k, n)

    barrier = pltpu.get_barrier_semaphore()
    for k in range(1, n):
        pl.semaphore_signal(barrier, inc=1, device_id={"slab": peer(k)}, device_id_type=MESH)

    def weight_copy(kind, layer):
        source, target = ((wr_hbm, wr), (ws_hbm, ws), (we_hbm, we))[kind]
        return pltpu.make_async_copy(source.at[layer], target.at[layer], w_sem.at[kind, layer])

    def x_copy(row):
        return pltpu.make_async_copy(x_hbm.at[row], x.at[row], x_sem.at[row])

    def out_copy(chunk):
        cols = pl.ds(chunk * mid, mid)
        return pltpu.make_async_copy(x.at[:, :, cols], out_hbm.at[:, :, cols], out_sem.at[chunk])

    weight_copy(0, 0).start()
    for row in range(rows):
        x_copy(row).start()

    def stat_copy(stage, k):
        return pltpu.make_async_remote_copy(
            src_ref=stat_out.at[stage],
            dst_ref=stat.at[stage, me],
            send_sem=stat_send.at[stage, k],
            recv_sem=stat_recv.at[stage, me],
            device_id={"slab": peer(k)},
            device_id_type=MESH,
        )

    def stat_arrival(stage, k):
        source = peer(k)
        return pltpu.make_async_remote_copy(
            src_ref=stat_out.at[stage],
            dst_ref=stat.at[stage, source],
            send_sem=stat_send.at[stage, k],
            recv_sem=stat_recv.at[stage, source],
            device_id={"slab": source},
            device_id_type=MESH,
        )

    def fold(carry, y):
        total, squares = carry
        y = y.reshape(-1, 8, mid)
        return total + jnp.sum(y, axis=0), squares + jnp.sum(y * y, axis=0)

    def zeros():
        return jnp.zeros((8, mid), jnp.float32), jnp.zeros((8, mid), jnp.float32)

    def send_stats(stage, carry):
        total = jnp.sum(carry[0], axis=0, keepdims=True)
        squares = jnp.sum(carry[1], axis=0, keepdims=True)
        both = jnp.concatenate([total, squares], axis=0)
        stat_out[stage] = both
        stat[stage, me] = both
        for k in range(1, n):
            stat_copy(stage, k).start()
        return total

    def affine(stage, gain, shift):
        for k in range(1, n):
            stat_copy(stage, k).wait_send()
            stat_arrival(stage, k).wait_recv()
        both = jnp.sum(stat[stage], axis=0)
        mean = both[0:1] * inv_count
        var = jnp.maximum(both[1:2] * inv_count - mean * mean, 0.0)
        scale = lax.rsqrt(var + EPS) * gain
        return scale, shift - mean * scale

    def halo_copy(layer, side):
        return pltpu.make_async_remote_copy(
            src_ref=halo_out.at[layer, side],
            dst_ref=halo_in.at[layer, 1 - side],
            send_sem=halo_send.at[layer, side],
            recv_sem=halo_recv.at[layer, 1 - side],
            device_id={"slab": peer(n - 1 if side == 0 else 1)},
            device_id_type=MESH,
        )

    def halo_arrival(layer, side):
        return pltpu.make_async_remote_copy(
            src_ref=halo_out.at[layer, side],
            dst_ref=halo_in.at[layer, side],
            send_sem=halo_send.at[layer, side],
            recv_sem=halo_recv.at[layer, side],
            device_id={"slab": peer(n - 1 if side == 0 else 1)},
            device_id_type=MESH,
        )

    def has_neighbour(side):
        return me > 0 if side == 0 else me < n - 1

    column = lax.broadcasted_iota(jnp.int32, (width, mid), 0)

    def store_taps(row, h):
        at = pl.ds(row * width, width)
        before = jnp.where(column == 0, 0.0, pltpu.roll(h, 1, 0))
        after = jnp.where(column == width - 1, 0.0, pltpu.roll(h, width - 1, 0))
        taps[at, 0:mid] = before.astype(jnp.bfloat16)
        taps[at, mid : 2 * mid] = h.astype(jnp.bfloat16)
        taps[at, 2 * mid : 3 * mid] = after.astype(jnp.bfloat16)

    def layer_step(layer, _):
        first = layer * stages

        weight_copy(0, layer).wait()

        def reduce_step(i, carry):
            @pl.when(layer == 0)
            def _():
                for r in range(step):
                    x_copy(i * step + r).wait()

            y = jnp.dot(
                x[pl.ds(i * step, step)].reshape(step * width, chans),
                wr[layer],
                preferred_element_type=jnp.float32,
            )
            red[pl.ds(i * step * width, step * width), :] = y
            return fold(carry, y)

        carry = lax.fori_loop(0, rows // step, reduce_step, zeros())

        @pl.when(layer == 0)
        def _():
            pl.semaphore_wait(barrier, n - 1)

        local_mean = send_stats(first, carry) * inv_local
        for side in range(2):
            row = 0 if side == 0 else rows - 1
            halo_out[layer, side] = (red[row * width : (row + 1) * width, :] - local_mean).astype(
                jnp.bfloat16
            )

            @pl.when(has_neighbour(side))
            def _():
                halo_copy(layer, side).start()

        weight_copy(1, layer).start()
        weight_copy(2, layer).start()

        @pl.when(layer < layers - 1)
        def _():
            weight_copy(0, layer + 1).start()

        scale, shift = affine(first, gain_mid[layer, 0:1], shift_mid[layer, 0:1])

        def hidden_step(i, _):
            y = red[pl.ds(i * width, width), :]
            store_taps(i + 1, jnp.maximum(y * scale + shift, 0.0))
            return 0

        lax.fori_loop(0, rows, hidden_step, 0)

        weight_copy(1, layer).wait()

        def conv(row, count):
            total = None
            for down in range(3):
                part = jnp.dot(
                    taps[pl.ds((row + down) * width, count * width), :],
                    ws[layer, pl.ds(3 * down, 3)].reshape(3 * mid, mid),
                    preferred_element_type=jnp.float32,
                )
                total = part if total is None else total + part
            red[pl.ds(row * width, count * width), :] = total
            return total

        def inside_step(i, carry):
            return fold(carry, conv(1 + i * step, step))

        carry = lax.fori_loop(0, (rows - 2) // step, inside_step, zeros())

        for side in range(2):
            source = peer(n - 1 if side == 0 else 1)
            row = 0 if side == 0 else rows + 1

            @pl.when(has_neighbour(side))
            def _():
                halo_copy(layer, side).wait_send()
                halo_arrival(layer, side).wait_recv()
                theirs = stat[first, source][0:1] * inv_local
                y = halo_in[layer, side].astype(jnp.float32) + theirs
                store_taps(row, jnp.maximum(y * scale + shift, 0.0))

            @pl.when(jnp.logical_not(has_neighbour(side)))
            def _():
                taps[pl.ds(row * width, width), :] = jnp.zeros((width, 3 * mid), jnp.bfloat16)

        def edge_step(i, carry):
            return fold(carry, conv(i * (rows - 1), 1))

        carry = lax.fori_loop(0, 2, edge_step, carry)
        send_stats(first + 1, carry)

        scale, shift = affine(first + 1, gain_mid[layer, 1:2], shift_mid[layer, 1:2])

        def inner_step(i, _):
            at = pl.ds(i * width, width)
            inner[at, :] = jnp.maximum(red[at, :] * scale + shift, 0.0).astype(jnp.bfloat16)
            return 0

        lax.fori_loop(0, rows, inner_step, 0)

        weight_copy(2, layer).wait()
        for c in range(chunks):
            cols = slice(c * mid, (c + 1) * mid)

            def expand_step(i, carry):
                at = pl.ds(i * step * width, step * width)
                y = jnp.dot(
                    inner[at, :], we[layer, :, cols], preferred_element_type=jnp.float32
                )
                expanded[at, cols] = y
                return fold(carry, y)

            send_stats(first + 2 + c, lax.fori_loop(0, rows // step, expand_step, zeros()))

        for c in range(chunks):
            cols = slice(c * mid, (c + 1) * mid)
            scale, shift = affine(
                first + 2 + c,
                gain_out[pl.ds(layer, 1), cols],
                shift_out[pl.ds(layer, 1), cols],
            )

            def output_step(i, _):
                y = expanded[pl.ds(i * width, width), cols] * scale + shift
                y = y + x[i, :, cols].astype(jnp.float32)
                x[i, :, cols] = jnp.maximum(y, 0.0).astype(jnp.bfloat16)
                return 0

            lax.fori_loop(0, rows, output_step, 0)

            @pl.when(layer == layers - 1)
            def _():
                out_copy(c).start()

        return 0

    lax.fori_loop(0, layers, layer_step, 0)
    for c in range(chunks):
        out_copy(c).wait()


def solution(mesh):
    n = mesh.shape["slab"]

    def local(section_input, w_reduce, w_spatial, w_expand, gain_mid, shift_mid, gain_out, shift_out):
        rows, width, chans = section_input.shape
        layers, _, mid = w_reduce.shape
        chunks = chans // mid
        total = layers * (2 + chunks)
        bf16, f32 = jnp.bfloat16, jnp.float32
        hbm = pl.BlockSpec(memory_space=pl.ANY)
        vmem = pl.BlockSpec(memory_space=pltpu.VMEM)
        return pl.pallas_call(
            functools.partial(kernel, n),
            out_shape=jax.ShapeDtypeStruct(section_input.shape, bf16),
            in_specs=[hbm] * 4 + [vmem] * 4,
            out_specs=hbm,
            scratch_shapes=[
                pltpu.VMEM((rows, width, chans), bf16),
                pltpu.VMEM(w_reduce.shape, bf16),
                pltpu.VMEM(w_spatial.shape, bf16),
                pltpu.VMEM(w_expand.shape, bf16),
                pltpu.VMEM((rows * width, mid), f32),
                pltpu.VMEM(((rows + 2) * width, 3 * mid), bf16),
                pltpu.VMEM((rows * width, mid), bf16),
                pltpu.VMEM((rows * width, chans), f32),
                pltpu.VMEM((layers, 2, width, mid), bf16),
                pltpu.VMEM((layers, 2, width, mid), bf16),
                pltpu.VMEM((total, 2, mid), f32),
                pltpu.VMEM((total, n, 2, mid), f32),
                pltpu.SemaphoreType.DMA((rows,)),
                pltpu.SemaphoreType.DMA((3, layers)),
                pltpu.SemaphoreType.DMA((chunks,)),
                pltpu.SemaphoreType.DMA((layers, 2)),
                pltpu.SemaphoreType.DMA((layers, 2)),
                pltpu.SemaphoreType.DMA((total, n)),
                pltpu.SemaphoreType.DMA((total, n)),
            ],
            compiler_params=pltpu.CompilerParams(
                collective_id=0, has_side_effects=True, vmem_limit_bytes=56 * 1024 * 1024
            ),
            name="blocks",
        )(section_input, w_reduce, w_spatial, w_expand, gain_mid, shift_mid, gain_out, shift_out)

    placed = (P(("img", "slab"), None, None), P(), P(), P(), P(), P(), P(), P())
    return jax.shard_map(
        local, mesh=mesh, in_specs=placed, out_specs=P(("img", "slab"), None, None), check_vma=False
    )
```

time: 331 us -> 85 us (0.26)
  blocking collectives: 170 us -> 0 us
  Pallas kernels: 0 us -> 80.1 us
  matrix products: 62.1 us -> 0 us
  waiting for transfers between devices: 39.5 us -> 0 us
  other arithmetic: 25.5 us -> 0 us
  starting transfers between devices: 14.4 us -> 0 us
  local copies, waits for them, and re-layouts: 16.9 us -> 4.64 us
    psum x9 -> x0, blocking collectives: 170 us -> none  [batch_stats(): lax.psum((jnp.sum(values, axis=0), jnp.sum(values * values, axis=0)), 'sl...]
    pallas_call x0 -> x1, Pallas kernels: none -> 80.1 us  [local(): pl.pallas_call(functools.partial(kernel, n), out_shape=jax.ShapeDtypeStru...]
    dot_general x33 -> x0, matrix products: 62.1 us -> none  [the longest x27 37 us: spatial_conv(): jnp.dot(window, taps[3 * down + across], preferred_element_type=jnp.float32)]
    ppermute x6 -> x0, waiting for transfers between devices: 39.5 us -> none  [the longest x3 39.5 us: with_halo(): lax.ppermute(lax.slice_in_dim(block, block.shape[dim] - width, None, axis...]
    convert_element_type x6 -> x0, other arithmetic: 20.3 us -> none  [the longest x3 18.5 us: local(): jnp.maximum(summed, 0.0).astype(jnp.bfloat16).reshape(rows, width, chans)]
    slice x10 -> x0, local copies, waits for them, and re-layouts: 16.9 us -> none  [the longest x3 12.2 us: spatial_conv(): window = padded[down:down + rows, across:across + width].reshape(-1, mid)]
    ppermute x6 -> x0, starting transfers between devices: 14.4 us -> none  [the longest x3 10.1 us: with_halo(): lax.ppermute(lax.slice_in_dim(block, block.shape[dim] - width, None, axis...]
    unnamed x4 -> x1, local copies, waits for them, and re-layouts: 0.01 us -> 4.64 us
  transfers between devices with their start and end apart: 6 -> 0, of which waited for: 3 -> 0; matrix products, arithmetic and copies ran while one was open for 1% -> 0% of each run, Pallas kernels for 0% -> 0%
where the time goes in v1:
time: 85 us; the launch traced here: 84.8 us
  Pallas kernels  80.1 us (94%)
  local copies, waits for them, and re-layouts  4.64 us (5%)
    pallas_call x1, Pallas kernels, local(): pl.pallas_call(functools.partial(kernel, n), out_shape=jax.ShapeDtypeStru...  80.1 us
    unnamed x1, local copies, waits for them, and re-layouts  4.64 us

profile of v1, /device:TPU:0, one launch (start us, length us, event | category | flops | bytes accessed | tf_op | source)
XLA Modules:
  0.0 84.8 jit_solution(12680287487228438682)
XLA Ops:
  0.0 80.1 %blocks.1 = bf16[8,256,1024]{2,1,0:T(8,128)(2,1)} custom-call(bf16[8,256,1024]{2,1,0:T(8,128)(2,1)} %x_hbm.1, bf16[3,1024,256]{2,1,0:T(8,128)(2,1)} %wr_hbm.1, bf16[3,9,256,256]{3,2,1,0:T(8,128)(2,1)} %ws_hbm.1, bf16[3,256,1024]{2,1,0:T(8,128)(2,1)} %we_hbm.1, f32[3,2,256]{2,1,0:T(2,128)} %gain_mid.1, f32[3,2,256]{2,1,0:T(2,128)} %shift_mid.1, ...), custom_call_target="tpu_custom_call" | custom-call | tf_op jit(solution)/shard_map/blocks/pallas_call | solution.py:286
  80.1 4.6 %copy.10 = bf16[8,256,1024]{2,1,0:T(8,128)(2,1)} copy(bf16[8,256,1024]{2,1,0:T(8,128)(2,1)} %blocks.1) | data formatting | bytes 8388608

commit v2 on v1

--- a/solution.py
+++ b/solution.py
@@ -9,18 +9,29 @@
 
 MESH = pl.DeviceIdType.MESH
 EPS = 1e-05
+REDUCE_ROWS = 2
+CONV_ROWS = 6
+EXPAND_ROWS = 8
+OUTPUT_ROWS = 4
+
+
+def divisor(rows, most):
+    return max(d for d in range(1, most + 1) if rows % d == 0)
 
 
 def kernel(
     n, x_hbm, wr_hbm, ws_hbm, we_hbm, gain_mid, shift_mid, gain_out, shift_out, out_hbm,
-    x, wr, ws, we, red, taps, inner, expanded, halo_out, halo_in, stat_out, stat,
+    x, wr, ws, we, red, taps, inner, expanded, halo_out, halo_in, stat_out, stat, sums,
     x_sem, w_sem, out_sem, halo_send, halo_recv, stat_send, stat_recv,
 ):
     rows, width, chans = x.shape
     layers, _, mid = wr.shape
     chunks = chans // mid
     stages = 2 + chunks
-    step = 2 if rows % 2 == 0 else 1
+    reduce_rows = divisor(rows, REDUCE_ROWS)
+    conv_rows = divisor(rows - 2, CONV_ROWS)
+    expand_rows = divisor(rows, EXPAND_ROWS)
+    output_rows = divisor(rows, OUTPUT_ROWS)
     me = lax.axis_index("slab")
     inv_local = 1.0 / (rows * width)
     inv_count = 1.0 / (rows * width * n)
@@ -129,31 +140,29 @@
         taps[at, mid : 2 * mid] = h.astype(jnp.bfloat16)
         taps[at, 2 * mid : 3 * mid] = after.astype(jnp.bfloat16)
 
+    def keep_sums(carry):
+        sums[0] = carry[0]
+        sums[1] = carry[1]
+
+    def reduce_step(i, carry):
+        for r in range(reduce_rows):
+            x_copy(i * reduce_rows + r).wait()
+        y = jnp.dot(
+            x[pl.ds(i * reduce_rows, reduce_rows)].reshape(reduce_rows * width, chans),
+            wr[0],
+            preferred_element_type=jnp.float32,
+        )
+        red[pl.ds(i * reduce_rows * width, reduce_rows * width), :] = y
+        return fold(carry, y)
+
+    weight_copy(0, 0).wait()
+    keep_sums(lax.fori_loop(0, rows // reduce_rows, reduce_step, zeros()))
+    pl.semaphore_wait(barrier, n - 1)
+
     def layer_step(layer, _):
         first = layer * stages
 
-        weight_copy(0, layer).wait()
-
-        def reduce_step(i, carry):
-            @pl.when(layer == 0)
-            def _():
-                for r in range(step):
-                    x_copy(i * step + r).wait()
-
-            y = jnp.dot(
-                x[pl.ds(i * step, step)].reshape(step * width, chans),
-                wr[layer],
-                preferred_element_type=jnp.float32,
-            )
-            red[pl.ds(i * step * width, step * width), :] = y
-            return fold(carry, y)
-
-        carry = lax.fori_loop(0, rows // step, reduce_step, zeros())
-
-        @pl.when(layer == 0)
-        def _():
-            pl.semaphore_wait(barrier, n - 1)
-
+        carry = (sums[0], sums[1])
         local_mean = send_stats(first, carry) * inv_local
         for side in range(2):
             row = 0 if side == 0 else rows - 1
@@ -196,9 +205,9 @@
             return total
 
         def inside_step(i, carry):
-            return fold(carry, conv(1 + i * step, step))
-
-        carry = lax.fori_loop(0, (rows - 2) // step, inside_step, zeros())
+            return fold(carry, conv(1 + i * conv_rows, conv_rows))
+
+        carry = lax.fori_loop(0, (rows - 2) // conv_rows, inside_step, zeros())
 
         for side in range(2):
             source = peer(n - 1 if side == 0 else 1)
@@ -224,26 +233,26 @@
 
         scale, shift = affine(first + 1, gain_mid[layer, 1:2], shift_mid[layer, 1:2])
 
-        def inner_step(i, _):
-            at = pl.ds(i * width, width)
-            inner[at, :] = jnp.maximum(red[at, :] * scale + shift, 0.0).astype(jnp.bfloat16)
-            return 0
-
-        lax.fori_loop(0, rows, inner_step, 0)
-
         weight_copy(2, layer).wait()
         for c in range(chunks):
             cols = slice(c * mid, (c + 1) * mid)
 
             def expand_step(i, carry):
-                at = pl.ds(i * step * width, step * width)
-                y = jnp.dot(
-                    inner[at, :], we[layer, :, cols], preferred_element_type=jnp.float32
-                )
-                expanded[at, cols] = y
+                at = pl.ds(i * expand_rows * width, expand_rows * width)
+                if c == 0:
+                    block = jnp.maximum(red[at, :] * scale + shift, 0.0).astype(jnp.bfloat16)
+                    inner[at, :] = block
+                else:
+                    block = inner[at, :]
+                y = jnp.dot(block, we[layer, :, cols], preferred_element_type=jnp.float32)
+                expanded[c, at, :] = y
                 return fold(carry, y)
 
-            send_stats(first + 2 + c, lax.fori_loop(0, rows // step, expand_step, zeros()))
+            send_stats(first + 2 + c, lax.fori_loop(0, rows // expand_rows, expand_step, zeros()))
+
+        @pl.when(layer < layers - 1)
+        def _():
+            weight_copy(0, layer + 1).wait()
 
         for c in range(chunks):
             cols = slice(c * mid, (c + 1) * mid)
@@ -253,16 +262,40 @@
                 shift_out[pl.ds(layer, 1), cols],
             )
 
-            def output_step(i, _):
-                y = expanded[pl.ds(i * width, width), cols] * scale + shift
-                y = y + x[i, :, cols].astype(jnp.float32)
-                x[i, :, cols] = jnp.maximum(y, 0.0).astype(jnp.bfloat16)
-                return 0
-
-            lax.fori_loop(0, rows, output_step, 0)
+            def output(row, count):
+                at = pl.ds(row * width, count * width)
+                y = expanded[c, at, :] * scale + shift
+                y = y + x[pl.ds(row, count), :, cols].reshape(count * width, mid).astype(jnp.float32)
+                y = jnp.maximum(y, 0.0).astype(jnp.bfloat16)
+                x[pl.ds(row, count), :, cols] = y.reshape(count, width, mid)
+                return y
+
+            @pl.when(layer < layers - 1)
+            def _():
+                def output_step(i, carry):
+                    at = pl.ds(i * output_rows * width, output_rows * width)
+                    y = jnp.dot(
+                        output(i * output_rows, output_rows),
+                        wr[layer + 1, cols, :],
+                        preferred_element_type=jnp.float32,
+                    )
+                    if c > 0:
+                        y = y + red[at, :]
+                    red[at, :] = y
+                    return fold(carry, y) if c == chunks - 1 else carry
+
+                if c == chunks - 1:
+                    keep_sums(lax.fori_loop(0, rows // output_rows, output_step, zeros()))
+                else:
+                    lax.fori_loop(0, rows // output_rows, output_step, 0)
 
             @pl.when(layer == layers - 1)
             def _():
+                def output_step(i, _):
+                    output(i, 1)
+                    return 0
+
+                lax.fori_loop(0, rows, output_step, 0)
                 out_copy(c).start()
 
         return 0
@@ -296,11 +329,12 @@
                 pltpu.VMEM((rows * width, mid), f32),
                 pltpu.VMEM(((rows + 2) * width, 3 * mid), bf16),
                 pltpu.VMEM((rows * width, mid), bf16),
-                pltpu.VMEM((rows * width, chans), f32),
+                pltpu.VMEM((chunks, rows * width, mid), f32),
                 pltpu.VMEM((layers, 2, width, mid), bf16),
                 pltpu.VMEM((layers, 2, width, mid), bf16),
                 pltpu.VMEM((total, 2, mid), f32),
                 pltpu.VMEM((total, n, 2, mid), f32),
+                pltpu.VMEM((2, 8, mid), f32),
                 pltpu.SemaphoreType.DMA((rows,)),
                 pltpu.SemaphoreType.DMA((3, layers)),
                 pltpu.SemaphoreType.DMA((chunks,)),

time: 85 us -> 76.2 us (0.90)
  Pallas kernels: 80.1 us -> 71.3 us
    pallas_call x1, Pallas kernels: 80.1 us -> 71.3 us  [local(): pl.pallas_call(functools.partial(kernel, n), out_shape=jax.ShapeDtypeStru...]
where the time goes in v2:
time: 76.2 us; the launch traced here: 75.9 us
  Pallas kernels  71.3 us (94%)
  local copies, waits for them, and re-layouts  4.64 us (6%)
    pallas_call x1, Pallas kernels, local(): pl.pallas_call(functools.partial(kernel, n), out_shape=jax.ShapeDtypeStru...  71.3 us
    unnamed x1, local copies, waits for them, and re-layouts  4.64 us

profile of v2, /device:TPU:0, one launch (start us, length us, event | category | flops | bytes accessed | tf_op | source)
XLA Modules:
  0.0 75.9 jit_solution(1870778041020003890)
XLA Ops:
  0.0 71.3 %blocks.1 = bf16[8,256,1024]{2,1,0:T(8,128)(2,1)} custom-call(bf16[8,256,1024]{2,1,0:T(8,128)(2,1)} %x_hbm.1, bf16[3,1024,256]{2,1,0:T(8,128)(2,1)} %wr_hbm.1, bf16[3,9,256,256]{3,2,1,0:T(8,128)(2,1)} %ws_hbm.1, bf16[3,256,1024]{2,1,0:T(8,128)(2,1)} %we_hbm.1, f32[3,2,256]{2,1,0:T(2,128)} %gain_mid.1, f32[3,2,256]{2,1,0:T(2,128)} %shift_mid.1, ...), custom_call_target="tpu_custom_call" | custom-call | tf_op jit(solution)/shard_map/blocks/pallas_call | solution.py:319
  71.3 4.6 %copy.10 = bf16[8,256,1024]{2,1,0:T(8,128)(2,1)} copy(bf16[8,256,1024]{2,1,0:T(8,128)(2,1)} %blocks.1) | data formatting | bytes 8388608
